TPU v7x, 32 devices: a 4x2x2 block of a 4x4x8 slice. The times are simulated.
32 devices in a mesh: batch: 4 (over y, z), seq: 8 (over x, core).
Axes of the slice: x: 4, y: 2, z: 2, core: 2. Of those that a mesh axis runs over, the one named last changes fastest.
The devices are a block of a 4x4x8 slice.
Arguments:
- hidden: bfloat16 [64, 5120], P('batch'), parts along dimension 0
- lengths: int32 [64], P('batch'), parts along dimension 0
- c_kv: bfloat16 [64, 8192, 512], P('batch', 'seq'), parts along dimension 0
- k_rope: bfloat16 [64, 8192, 64], P('batch', 'seq'), parts along dimension 0
- w_uq: bfloat16 [5120, 128, 128], P(None, 'seq')
- w_qr: bfloat16 [5120, 128, 64], P(None, 'seq')
- w_uk: bfloat16 [128, 128, 512], P('seq')
- w_uv: bfloat16 [128, 512, 128], P('seq')
- w_o: bfloat16 [128, 128, 5120], P('seq')
Outputs:
- output: bfloat16 [64, 5120], P('batch'), parts along dimension 0
There are 4 independent parts. A program takes and returns all parts, laid end to end along the dimension named above; an argument that names none is the same for every part.
All inputs are finite; a program needn't handle non-finite values.
Results may differ from a plain program's by a relative error of at most 0.00434223.
Values are sent between devices in bfloat16 or wider.
A program may use at most 768 MiB of HBM per device.

v0:
```python
import math
import jax
import jax.numpy as jnp
from jax import lax
from jax.sharding import PartitionSpec as P


def solution(mesh):
    row_spec = P('batch', None)
    cache_spec = P('batch', 'seq', None)
    in_specs = (row_spec, P('batch'), cache_spec, cache_spec, P(None, 'seq', None), P(None, 'seq', None), P('seq', None, None), P('seq', None, None), P('seq', None, None))

    def mla_step(hidden, lengths, c_kv, k_rope, w_uq, w_qr, w_uk, w_uv, w_o):
        shard_len = c_kv.shape[1]
        lat_dim = c_kv.shape[2]
        score_scale = 1.0 / math.sqrt(w_uq.shape[2] + w_qr.shape[2])
        q_nope = jnp.einsum('bd,dhk->bhk', hidden, w_uq, preferred_element_type=jnp.float32).astype(jnp.bfloat16)
        q_rope = jnp.einsum('bd,dhr->bhr', hidden, w_qr, preferred_element_type=jnp.float32).astype(jnp.bfloat16)
        q_lat = jnp.einsum('bhk,hkc->bhc', q_nope, w_uk, preferred_element_type=jnp.float32).astype(jnp.bfloat16)
        q_local = jnp.concatenate([q_lat, q_rope], axis=2)
        q_all = lax.all_gather(q_local, 'seq', axis=1, tiled=True)
        scores = (jnp.einsum('bhc,btc->bht', q_all[:, :, :lat_dim], c_kv, preferred_element_type=jnp.float32) + jnp.einsum('bhr,btr->bht', q_all[:, :, lat_dim:], k_rope, preferred_element_type=jnp.float32)) * score_scale
        positions = lax.axis_index('seq') * shard_len + jnp.arange(shard_len)
        is_valid = positions[None, None, :] < lengths[:, None, None]
        scores = jnp.where(is_valid, scores, -jnp.inf)
        local_max = jnp.max(scores, axis=2)
        exp_shift = jnp.where(local_max > -jnp.inf, local_max, 0.0)
        p_weights = jnp.exp(scores - exp_shift[:, :, None])
        weight_sum = jnp.sum(p_weights, axis=2)
        latent_sum = jnp.einsum('bht,btc->bhc', p_weights.astype(jnp.bfloat16), c_kv, preferred_element_type=jnp.float32)
        global_max = lax.pmax(local_max, 'seq')
        rescale = jnp.exp(local_max - global_max)
        packed = jnp.concatenate([latent_sum * rescale[:, :, None], (weight_sum * rescale)[:, :, None]], axis=2)
        merged = lax.psum_scatter(packed, 'seq', scatter_dimension=1, tiled=True)
        o_lat = (merged[:, :, :lat_dim] / merged[:, :, lat_dim:]).astype(jnp.bfloat16)
        o_val = jnp.einsum('bhc,hcv->bhv', o_lat, w_uv, preferred_element_type=jnp.float32).astype(jnp.bfloat16)
        y_part = jnp.einsum('bhv,hvd->bd', o_val, w_o, preferred_element_type=jnp.float32)
        y_sum = lax.psum(y_part, 'seq')
        return (hidden.astype(jnp.float32) + y_sum).astype(jnp.bfloat16)

    return jax.shard_map(mla_step, mesh=mesh, in_specs=in_specs, out_specs=row_spec, check_vma=False)
```

profile of v0, /device:TPU:81, one launch (start us, length us, event | category | flops | bytes accessed | tf_op | source)
XLA Modules:
  0.0 223.5 jit_solution(8063681511854061791)
XLA Ops:
  6.5 0.0 copy-start
  6.6 0.0 copy-start.3
  6.6 0.0 all-gather.2.cloned.1.call-start
  6.6 8.4 %convolution_convert_fusion.2 = bf16[16,16,64]{2,0,1:T(8,128)(2,1)S(1)} fusion(bf16[5120,16,64]{0,2,1:T(8,128)(2,1)} %param.14, bf16[16,5120]{1,0:T(8,128)(2,1)} %param.9), kind=kOutput, calls=%fused_computation.20 | convolution fusion | flops 167788544 | bytes 10682368 | tf_op jit(solution)/shard_map/bd,dhr->bhr/dot_general | solution.py:18
  14.9 0.0 copy-done.3
  14.9 0.0 copy-start.4
  14.9 10.7 %fusion.14 = bf16[16,16,512]{2,0,1:T(8,128)(2,1)S(1)} fusion(bf16[16,128,512]{2,1,0:T(8,128)(2,1)} %param.15, bf16[5120,16,128]{2,1,0:T(8,128)(2,1)} %param.13, bf16[16,5120]{1,0:T(8,128)(2,1)S(1)} %copy-done.3), kind=kOutput, calls=%fused_computation.17 | convolution fusion | flops 369262592 | bytes 23494656 | tf_op jit(solution)/shard_map/bhk,hkc->bhc/dot_general | solution.py:19
  25.6 0.8 pad_maximum_fusion.1
  26.4 0.1 all-gather.2.cloned.1.call-update
  26.5 0.1 reduce-scatter.2.cloned.1.call-start
  26.6 0.0 copy-done.4
  26.6 0.1 broadcast_compare_fusion
  26.7 27.5 %all-gather.2.cloned.1.call-done = bf16[16,128,576]{2,0,1:T(8,128)(2,1)} async-done(((bf16[16,16,576]{2,0,1:T(8,128)(2,1)}), bf16[16,128,576]{2,0,1:T(8,128)(2,1)}) %all-gather.2.cloned.1.call-update) | async-done | bytes 2359312 | tf_op jit(solution)/shard_map/all_gather | solution.py:21
  54.1 0.0 copy-start.2
  54.1 1.2 slice.17
  55.4 0.0 copy-done
  55.4 4.5 %fusion.22 = f32[16,128,1024]{2,1,0:T(8,128)} fusion(bf16[16,1024,64]{1,2,0:T(8,128)(2,1)S(1)} %copy-done, bf16[16,128,64]{2,0,1:T(8,128)(2,1)S(1)} %slice.17), kind=kOutput, calls=%fused_computation.24 | convolution fusion | flops 268435456 | bytes 10747904 | tf_op jit(solution)/shard_map/bhr,btr->bht/dot_general | solution.py:22
  59.8 0.0 copy-done.2
  59.8 0.3 slice.16
  60.1 13.4 %fusion.7 = (f32[16,128]{1,0:T(8,128)S(1)}, f32[16,128,1024]{2,1,0:T(8,128)}) fusion(f32[16,128,1024]{2,1,0:T(8,128)} %fusion.22, pred[16,1024]{1,0:T(8,128)(4,1)S(1)} %broadcast_compare_fusion, bf16[16,1024,512]{2,1,0:T(8,128)(2,1)} %param.11, bf16[16,128,512]{2,0,1:T(8,128)(2,1)S(1)} %slice.16), kind=kOutput, calls=%fused_computation.10 | convolution fusion | flops 2155870208 | bytes 35676160 | tf_op jit(solution)/shard_map/bhc,btc->bht/dot_general | solution.py:22
  73.5 12.5 %pmax.7 = f32[16,128]{1,0:T(8,128)S(1)} all-reduce(f32[16,128]{1,0:T(8,128)S(1)} %get-tuple-element.7), channel_id=1, replica_groups=mesh['batch'=4,'seq'=8] {'seq'}, use_global_device_ids=true, to_apply=%region_1.2 | all-reduce | flops 2048 | bytes 16384 | tf_op jit(solution)/shard_map/pmax | solution.py:31
  86.0 0.0 slice-start
  86.0 0.0 slice-start.1
  86.0 7.7 %fusion.2 = f32[16,128]{1,0:T(8,128)S(1)} fusion(f32[16,128]{1,0:T(8,128)S(1)} %compare_select_fusion, f32[16,128,1024]{2,1,0:T(8,128)} %get-tuple-element.8, f32[16,128,1024]{2,1,0:T(8,128)} %fusion.22, pred[16,1024]{1,0:T(8,128)(4,1)S(1)} %broadcast_compare_fusion), kind=kLoop, calls=%fused_computation.4 | loop fusion | flops 10483712 | bytes 16809984 | tf_op jit(solution)/shard_map/reduce_sum | solution.py:29
  93.7 0.0 slice-done
  93.7 0.6 slice-done.1
  94.3 13.9 %broadcast_multiply_fusion = f32[16,128,512]{2,1,0:T(8,128)} fusion(f32[16,128]{1,0:T(8,128)S(1)} %get-tuple-element.6, bf16[16,1024,512]{2,1,0:T(8,128)(2,1)} %param.11, f32[16,128]{1,0:T(8,128)S(1)} %compare_select_fusion, f32[16,128,1024]{2,1,0:T(8,128)} %get-tuple-element.8, f32[16,128,1024]{2,1,0:T(8,128)S(1)} %bitcast.24, ...), kind=kOutput, calls=%fused_computation.15 | convolution fusion | flops 2159017984 | bytes 37781504 | tf_op jit(solution)/shard_map/bht,btc->bhc/dot_general | solution.py:30
  108.2 0.4 copy.18
  108.6 5.0 %pad_maximum_fusion = f32[16,128,513]{2,1,0:T(8,128)} fusion(f32[16,128,1]{2,1,0:T(8,128)S(1)} %copy.18, f32[16,128,512]{2,1,0:T(8,128)} %broadcast_multiply_fusion), kind=kLoop, calls=%fused_computation.7 | loop fusion | flops 1050624 | bytes 8404992 | tf_op jit(solution)/shard_map/concatenate | solution.py:33
  113.6 0.1 reduce-scatter.2.cloned.1.call-update
  113.7 0.1 all-reduce.2.cloned.1.call-start
  113.8 34.8 %reduce-scatter.2.cloned.1.call-done = f32[16,16,513]{2,1,0:T(8,128)} async-done(((f32[16,128,513]{2,1,0:T(8,128)}), f32[16,16,513]{2,1,0:T(8,128)}) %reduce-scatter.2.cloned.1.call-update) | async-done | bytes 525328 | tf_op jit(solution)/shard_map/reduce_scatter | solution.py:34
  148.6 1.0 slice_reduce_fusion
  149.6 0.0 copy-start.1
  149.6 1.3 fusion.21
  150.9 10.1 %convolution_bitcast_fusion = f32[16,5120]{1,0:T(8,128)} fusion(bf16[16,128,5120]{2,1,0:T(8,128)(2,1)} %param.17, bf16[16,512,128]{2,1,0:T(8,128)(2,1)} %param.16, bf16[16,16,512]{2,1,0:T(8,128)(2,1)S(1)} %fusion.21), kind=kOutput, calls=%fused_computation.6 | convolution fusion | flops 369131520 | bytes 23658496 | tf_op jit(solution)/shard_map/bhv,hvd->bd/dot_general | solution.py:37
  161.0 0.1 all-reduce.2.cloned.1.call-update
  161.1 54.2 %all-reduce.2.cloned.1.call-done = f32[16,5120]{1,0:T(8,128)} async-done(((f32[16,5120]{1,0:T(8,128)}), f32[16,5120]{1,0:T(8,128)}) %all-reduce.2.cloned.1.call-update) | async-done | bytes 327696 | tf_op jit(solution)/shard_map/psum | solution.py:38
  215.3 1.7 add_convert_fusion
  216.9 0.0 copy-done.1
  (4 shorter events, 0.0 us)
Async XLA Ops:
  6.5 48.8 %copy-start = (bf16[16,1024,64]{1,2,0:T(8,128)(2,1)S(1)}, bf16[16,1024,64]{1,2,0:T(8,128)(2,1)}, u32[]{:S(2)}) copy-start(bf16[16,1024,64]{1,2,0:T(8,128)(2,1)} %param.12) | copy-start | bytes 6291460
  6.6 8.4 %copy-start.3 = (bf16[16,5120]{1,0:T(8,128)(2,1)S(1)}, bf16[16,5120]{1,0:T(8,128)(2,1)}, u32[]{:S(2)}) copy-start(bf16[16,5120]{1,0:T(8,128)(2,1)} %param.9) | copy-start | bytes 491524
  6.6 47.6 %all-gather.2.cloned.1.call-start = ((), (), s32[]{:S(2)}) async-start(), calls=%async_computation.1 | async-start | bytes 2949120 | tf_op jit(solution)/shard_map/all_gather | solution.py:21
  14.9 11.6 %copy-start.4 = (s32[16]{0:T(128)S(1)}, s32[16]{0:T(128)}, u32[]{:S(2)}) copy-start(s32[16]{0:T(128)} %param.10) | copy-start | bytes 196
  26.5 122.1 %reduce-scatter.2.cloned.1.call-start = ((), (), s32[]{:S(2)}) async-start(), calls=%async_computation.2 | async-start | bytes 5898240 | tf_op jit(solution)/shard_map/reduce_scatter | solution.py:34
  54.1 5.7 %copy-start.2 = (bf16[16,128,576]{2,0,1:T(8,128)(2,1)S(1)}, bf16[16,128,576]{2,0,1:T(8,128)(2,1)}, u32[]{:S(2)}) copy-start(bf16[16,128,576]{2,0,1:T(8,128)(2,1)} %all-gather.2.cloned.1.call-done) | copy-start | bytes 7077892
  86.0 7.7 %slice-start = ((s8[8388608]{0:T(1024)(128)(4,1)}), s8[4194304]{0:T(1024)(128)(4,1)S(1)}, s32[]{:S(2)}) async-start(s8[8388608]{0:T(1024)(128)(4,1)} %bitcast.23), calls=%async_computation.4 | async-start | bytes 8388608
  86.0 8.3 %slice-start.1 = ((s8[8388608]{0:T(1024)(128)(4,1)}), s8[4194304]{0:T(1024)(128)(4,1)S(1)}, s32[]{:S(2)}) async-start(s8[8388608]{0:T(1024)(128)(4,1)} %bitcast.23), calls=%async_computation.5 | async-start | bytes 8388608
  113.7 101.6 %all-reduce.2.cloned.1.call-start = ((), (), s32[]{:S(2)}) async-start(), calls=%async_computation.3 | async-start | bytes 655360 | tf_op jit(solution)/shard_map/psum | solution.py:38
  149.6 67.3 %copy-start.1 = (bf16[16,1024,64]{1,2,0:T(8,128)(2,1)S(1)}, bf16[16,1024,64]{1,2,0:T(8,128)(2,1)}, u32[]{:S(2)}) copy-start(bf16[16,1024,64]{1,2,0:T(8,128)(2,1)} %param.12) | copy-start | bytes 6291460
Sparse Core Ops, SparseCore 0:
  26.6 27.4 all-gather.1
  113.8 34.7 reduce-scatter.1
  161.2 53.9 all-reduce.1
where the time goes:
time: 225 us; the launch traced here: 223 us
  waiting for transfers between devices  117 us (52%)
  matrix products  60.9 us (27%)
  other arithmetic  16.6 us (7%)
  between operations  13.3 us (6%)
  blocking collectives  12.5 us (6%)
  local copies, waits for them, and re-layouts  3.47 us (2%)
    psum x1, waiting for transfers between devices, mla_step(): y_sum = lax.psum(y_part, 'seq')  54.2 us
    reduce_scatter x1, waiting for transfers between devices, mla_step(): merged = lax.psum_scatter(packed, 'seq', scatter_dimension=1, tiled=True)  34.8 us
    all_gather x1, waiting for transfers between devices, mla_step(): q_all = lax.all_gather(q_local, 'seq', axis=1, tiled=True)  27.5 us
    dot_general x1, matrix products, mla_step(): jnp.einsum('bht,btc->bhc', p_weights.astype(jnp.bfloat16), c_kv, preferre...  13.9 us
    dot_general x1, matrix products, mla_step(): jnp.einsum('bhc,btc->bht', q_all[:, :, :lat_dim], c_kv, preferred_element...  13.4 us
    pmax x1, blocking collectives, mla_step(): global_max = lax.pmax(local_max, 'seq')  12.5 us
    dot_general x1, matrix products, mla_step(): jnp.einsum('bhk,hkc->bhc', q_nope, w_uk, preferred_element_type=jnp.float32)  10.7 us
    dot_general x1, matrix products, mla_step(): jnp.einsum('bhv,hvd->bd', o_val, w_o, preferred_element_type=jnp.float32)  10.1 us
  transfers between devices with their start and end apart: 3, of which 3 were waited for; matrix products, arithmetic and copies ran while one was open for 0% of the time, Pallas kernels for 0%

commit v1 on v0

v1 whole, which is shorter than its diff:
```python
import functools
import math

import jax
import jax.numpy as jnp
from jax import lax
from jax.experimental import pallas as pl
from jax.experimental.pallas import tpu as pltpu
from jax.sharding import PartitionSpec as P

MESH = pl.DeviceIdType.MESH
F32 = jnp.float32
BF16 = jnp.bfloat16
LOWEST = float(jnp.finfo(jnp.float32).min)
DCH = 256
SLOTS = 8
RPC = 2


def iota(shape, dim):
    return lax.broadcasted_iota(jnp.int32, shape, dim)


def dot(a, b):
    return lax.dot_general(a, b, (((1,), (0,)), ((), ())), preferred_element_type=F32)


def dot_nt(a, b):
    return lax.dot_general(a, b, (((1,), (1,)), ((), ())), preferred_element_type=F32)


def merge(blocks, lat):
    rows = []
    for r in range(RPC):
        base = RPC * lat
        ms = [b[:, base + r:base + r + 1] for b in blocks]
        ls = [b[:, base + RPC + r:base + RPC + r + 1] for b in blocks]
        m = functools.reduce(jnp.maximum, ms)
        ws = [jnp.exp(x - m) for x in ms]
        l = functools.reduce(lambda a, b: a + b, [w * y for w, y in zip(ws, ls)])
        o = functools.reduce(lambda a, b: a + b,
                             [w * b[:, r * lat:(r + 1) * lat] for w, b in zip(ws, blocks)])
        rows.append((o, m, l))
    return rows


def pack_ml(ms, ls, shape):
    lane = iota(shape, 1)
    out = jnp.zeros(shape, F32)
    for r in range(RPC):
        out = jnp.where(lane == r, ms[r], out)
        out = jnp.where(lane == RPC + r, ls[r], out)
    return out


def kernel(n, scale, lens, hid, c_hbm, k_hbm, wuq_hbm, wqr_hbm, wuk_hbm, wuv_hbm, wo_hbm, out_ref,
           hexp, wbuf, wuk, wuv, wo, cb, kb, acc, q_all, qr_st, qr_all, qrow, o_buf, d2d, mid, fin, ol, ovb,
           y_send, y_recv, y_own, out_all,
           w_sem, wuk_sem, wqr_sem, c_sem, k_sem, wuv_sem, wo_sem,
           ag_s, ag_r, rs_s, d2d_r, mid_r, fin_r, y_s, y_r, g_s, g_r):
    s = lax.axis_index("seq")
    x, c = lax.div(s, 2), lax.rem(s, 2)
    nx = n // 2
    oc = 1 - c
    xr, xl, xo = lax.rem(x + 1, nx), lax.rem(x + nx - 1, nx), lax.rem(x + 2, nx)
    partner, right, left = 2 * x + oc, 2 * xr + c, 2 * xl + c
    rows, dm = hid.shape
    t_len, lat = cb.shape[1], cb.shape[2]
    nheads = 16 * n
    nc = dm // DCH
    nch = rows // RPC

    def remote(src, dst, ssem, rsem, dev):
        return pltpu.make_async_remote_copy(src_ref=src, dst_ref=dst, send_sem=ssem, recv_sem=rsem,
                                            device_id={"seq": dev}, device_id_type=MESH)

    def w_copy(g):
        half, i = lax.div(g, nc), lax.rem(g, nc)
        return pltpu.make_async_copy(wuq_hbm.at[pl.ds(i * DCH, DCH), half], wbuf.at[lax.rem(g, SLOTS)],
                                     w_sem.at[lax.rem(g, SLOTS)])

    def wuk_copy(half):
        return pltpu.make_async_copy(wuk_hbm.at[half], wuk.at[half], wuk_sem.at[half])

    def wqr_copy(j):
        return pltpu.make_async_copy(wqr_hbm.at[pl.ds(j * 128, 128)], wo.at[pl.ds(j * 128, 128)], wqr_sem.at[j])

    def c_copy(b):
        return pltpu.make_async_copy(c_hbm.at[b], cb.at[b], c_sem.at[b])

    def k_copy(b):
        return pltpu.make_async_copy(k_hbm.at[b], kb.at[b], k_sem.at[b])

    def wo_copy(j):
        return pltpu.make_async_copy(wo_hbm.at[pl.ds(j * 256, 256)], wo.at[pl.ds(j * 256, 256)], wo_sem.at[j])

    wuk_copy(0).start()
    for g in range(SLOTS):
        w_copy(jnp.int32(g)).start()

    barrier = pltpu.get_barrier_semaphore()
    for d in range(1, n):
        pl.semaphore_signal(barrier, inc=1, device_id={"seq": lax.rem(s + d, n)}, device_id_type=MESH)

    rep = jnp.where(iota((128, 1024), 0) == lax.div(iota((128, 1024), 1), 8), 1.0, 0.0).astype(BF16)
    ndt = dm // 128
    for g0 in range(0, ndt, 8):
        grp = list(range(g0, min(g0 + 8, ndt)))
        st = jnp.concatenate([hid[:, t * 128:(t + 1) * 128] for t in grp], axis=0)
        ex = dot(st, rep).astype(BF16)
        for i, t in enumerate(grp):
            hexp[:, t * 1024:(t + 1) * 1024] = ex[i * 16:(i + 1) * 16]

    head_mask = jnp.where(lax.div(iota((128, 128), 0), 16) == lax.rem(iota((128, 128), 1), 8), 1.0, 0.0).astype(BF16)
    ri, ci = iota((128, 128), 0), iota((128, 128), 1)
    to_bh = jnp.where(ci == lax.rem(ri, 8) * 16 + lax.div(ri, 8), 1.0, 0.0).astype(BF16)
    to_hb = jnp.where(ci == lax.rem(ri, 16) * 8 + lax.div(ri, 16), 1.0, 0.0).astype(BF16)
    row_h = lax.rem(iota((128, 1), 0), 8)

    pl.semaphore_wait(barrier, n - 1)

    def ag_buf(t, owner):
        return qr_all.at[owner] if t == 2 else q_all.at[owner, t]

    def ag(t, i, owner, dev):
        return remote(ag_buf(t, owner), ag_buf(t, owner), ag_s.at[t, i], ag_r.at[t, owner], dev)

    def ag_own(t):
        ag(t, 0, s, right).start()
        ag(t, 1, s, left).start()
        ag(t, 2, s, partner).start()

    def ag_fwd1(t):
        ag(t, 0, left, right).wait_recv()
        ag(t, 3, left, partner).start()
        if t != 1:
            ag(t, 5, left, right).start()
        ag(t, 1, right, left).wait_recv()
        ag(t, 4, right, partner).start()
        if t == 1:
            ag(t, 5, right, left).start()

    opp = 2 * xo + c

    def ag_fwd2(t):
        ag(t, 5, opp, right).wait_recv()
        ag(t, 6, opp, partner).start()

    def ag_partner(t):
        for xx in (x, xl, xr, xo):
            ag(t, 2, 2 * xx + oc, partner).wait_recv()

    def ag_done(t):
        for i in range(7):
            ag(t, i, s, partner).wait_send()

    kk = DCH * 8
    def half_step(half):
        acc[...] = jnp.zeros_like(acc)

        @pl.loop(0, nc)
        def _(i):
            g = half * nc + i
            slot = lax.rem(g, SLOTS)
            w_copy(g).wait()
            wv = wbuf[slot].reshape(kk, 128)
            part = acc[...]
            for q0 in range(0, kk, 512):
                hx = hexp[:, pl.ds(pl.multiple_of(i * kk + q0, 512), 512)]
                lhs = jnp.concatenate([hx] * 8, axis=0) * jnp.concatenate([head_mask] * 4, axis=1)
                part += dot(lhs, wv[q0:q0 + 512])
            acc[...] = part

            @pl.when(g + SLOTS < 2 * nc)
            def _():
                w_copy(g + SLOTS).start()

            @pl.when(g >= 2 * nc - 8)
            def _():
                wqr_copy(g - (2 * nc - 8)).start()

            if half == 0:
                @pl.when(i == 4)
                def _():
                    wuk_copy(1).start()
            else:
                @pl.when(i == nc // 2 + 2)
                def _():
                    ag_fwd1(0)

                @pl.when(i == nc - 1)
                def _():
                    ag_fwd2(0)

        qn = dot(to_bh, acc[...].astype(BF16)).astype(BF16)
        wuk_copy(half).wait()
        ql = jnp.zeros((128, lat), F32)
        for h in range(8):
            ql += dot(jnp.where(row_h == h, qn, jnp.zeros_like(qn)), wuk[half, h * 128:(h + 1) * 128, :])
        q_all[s, half] = ql.astype(BF16)
        ag_own(half)

    half_step(0)
    half_step(1)

    @pl.loop(0, 8)
    def _(j):
        wqr_copy(j).wait()
        qr = dot_nt(hid[...], wo[pl.ds(pl.multiple_of(j * 128, 128), 128), :])
        qr_st[pl.ds(pl.multiple_of(j * 16, 16), 16), :] = qr.astype(BF16)
        for r in range(2):
            b = 2 * j + r
            c_copy(b).start()
            k_copy(b).start()

        @pl.when(j == 5)
        def _():
            ag_fwd1(1)

    qr_all[s] = dot(to_bh, qr_st[...]).astype(BF16)
    ag_own(2)
    pltpu.make_async_copy(wuv_hbm, wuv, wuv_sem).start()
    ag_fwd2(1)
    ag_fwd1(2)
    ag_fwd2(2)
    for t in range(3):
        ag_partner(t)

    dup = jnp.where(lax.div(iota((128, 64), 0), 2) == iota((128, 64), 1), 1.0, 0.0).astype(BF16)
    rope_mask = jnp.where(lax.rem(iota((128, 128), 0), 2) == lax.div(iota((128, 128), 1), 64), 1.0, 0.0)
    pos = s * t_len + iota((1, t_len), 1)
    width = RPC * lat + 128

    def attend(k):
        k16 = pl.ds(pl.multiple_of(k * 16, 16), 16)
        for p in range(n):
            qa = q_all[p, 0, k16, :].astype(F32)
            qb = q_all[p, 1, k16, :].astype(F32)
            for r in range(RPC):
                qrow[r, p * 16:(p + 1) * 16, :] = jnp.concatenate(
                    [qa[r * 8:(r + 1) * 8], qb[r * 8:(r + 1) * 8]], axis=0).astype(BF16)
        mls = []
        for r in range(RPC):
            b = k * RPC + r
            c_copy(b).wait()
            k_copy(b).wait()
            pairs = jnp.concatenate(
                [qr_all[p, k16, :].astype(F32)[r * 8:(r + 1) * 8] for p in range(n)], axis=0).astype(BF16)
            qr = (dot(dup, pairs) * rope_mask).astype(BF16)
            keys = kb[b]
            sc = dot_nt(qrow[r], cb[b]) + dot(qr, jnp.concatenate([keys, keys], axis=0))
            sc = jnp.where(pos < lens[b], sc * scale, -jnp.inf)
            m = jnp.maximum(jnp.max(sc, axis=1, keepdims=True), LOWEST)
            pw = jnp.exp(sc - m)
            l = jnp.sum(pw, axis=1, keepdims=True)
            o = dot(pw.astype(BF16), cb[b])
            for p in range(n):
                for ab in range(2):
                    h0 = p * 16 + ab * 8
                    o_buf[k, p % 2, p // 2, ab, :, r * lat:(r + 1) * lat] = o[h0:h0 + 8]
            mls.append((m, l))
        ml = pack_ml([a for a, _ in mls], [a for _, a in mls], (nheads, 128))
        for p in range(n):
            for ab in range(2):
                h0 = p * 16 + ab * 8
                o_buf[k, p % 2, p // 2, ab, :, RPC * lat:] = ml[h0:h0 + 8]

    def d2d_copy(k):
        return remote(o_buf.at[k, oc], d2d.at[k], rs_s.at[k, 0], d2d_r.at[k], partner)

    def hop_copies(k):
        return [
            remote(o_buf.at[k, c, xo, 1], mid.at[k, 0], rs_s.at[k, 1], mid_r.at[k, 0], right),
            remote(o_buf.at[k, c, xo, 0], mid.at[k, 1], rs_s.at[k, 2], mid_r.at[k, 1], left),
            remote(o_buf.at[k, c, xr, 0], fin.at[k, 0], rs_s.at[k, 3], fin_r.at[k, 0], right),
            remote(o_buf.at[k, c, xl, 1], fin.at[k, 1], rs_s.at[k, 4], fin_r.at[k, 1], left),
        ]

    def mid_copies(k):
        return [
            remote(o_buf.at[k, c, xr, 1], fin.at[k, 2], rs_s.at[k, 5], fin_r.at[k, 2], right),
            remote(o_buf.at[k, c, xl, 0], fin.at[k, 3], rs_s.at[k, 6], fin_r.at[k, 3], left),
        ]

    def store_merged(k, xx, ab, other):
        ref = o_buf.at[k, c, xx, ab]
        res = merge([ref[...], other], lat)
        for r in range(RPC):
            ref[:, r * lat:(r + 1) * lat] = res[r][0]
        ref[:, RPC * lat:] = pack_ml([a[1] for a in res], [a[2] for a in res], (8, 128))

    def pair_stage(k):
        d2d_copy(k).wait_recv()
        for xx in range(nx):
            for ab in range(2):
                store_merged(k, xx, ab, d2d[k, xx, ab])
        for cp in hop_copies(k):
            cp.start()

    def mid_stage(k):
        hops, mids = hop_copies(k), mid_copies(k)
        hops[0].wait_recv()
        store_merged(k, xr, 1, mid[k, 0])
        mids[0].start()
        hops[1].wait_recv()
        store_merged(k, xl, 0, mid[k, 1])
        mids[1].start()

    def final_stage(k):
        hops, mids = hop_copies(k), mid_copies(k)
        hops[2].wait_recv()
        hops[3].wait_recv()
        mids[0].wait_recv()
        mids[1].wait_recv()
        for ab, (f0, f1) in enumerate(((0, 3), (1, 2))):
            res = merge([o_buf[k, c, x, ab], fin[k, f0], fin[k, f1]], lat)
            ol[ab, pl.ds(pl.multiple_of(k * 16, 16), 16), :] = jnp.concatenate(
                [o / l for o, _, l in res], axis=0).astype(BF16)

    @pl.loop(0, nch + 3)
    def _(k):
        @pl.when(k < nch)
        def _():
            attend(k)
            d2d_copy(k).start()
            wo_copy(k).start()

        @pl.when((k >= 1) & (k < nch + 1))
        def _():
            pair_stage(k - 1)

        @pl.when((k >= 2) & (k < nch + 2))
        def _():
            mid_stage(k - 2)

        @pl.when(k >= 3)
        def _():
            final_stage(k - 3)

    pltpu.make_async_copy(wuv_hbm, wuv, wuv_sem).wait()
    for ab in range(2):
        ov = jnp.zeros((128, 128), F32)
        src = ol[ab]
        for h in range(8):
            ov += dot(jnp.where(row_h == h, src, jnp.zeros_like(src)), wuv[ab, h * lat:(h + 1) * lat, :])
        ov = dot(to_hb, ov.astype(BF16)).astype(BF16)
        for h in range(8):
            ovb[:, (ab * 8 + h) * 128:(ab * 8 + h + 1) * 128] = ov[h * 16:(h + 1) * 16]
    for j in range(8):
        wo_copy(j).wait()

    yw = dm // n

    def y_copy(d):
        dev = lax.rem(s + d, n)
        return remote(y_send.at[dev], y_recv.at[s], y_s.at[dev], y_r.at[s], dev)

    def y_wait(src):
        return remote(y_send.at[src], y_recv.at[src], y_s.at[src], y_r.at[src], src)

    @pl.loop(1, n + 1)
    def _(d):
        dev = lax.rem(s + d, n)
        y_send[dev] = dot(ovb[...], wo[:, pl.ds(pl.multiple_of(dev * yw, yw), yw)])

        @pl.when(d < n)
        def _():
            y_copy(d).start()

    y = y_send[s]
    for d in range(1, n):
        src = lax.rem(s + d, n)
        y_wait(src).wait_recv()
        y += y_recv[src]
    y += hid[:, pl.ds(pl.multiple_of(s * yw, yw), yw)].astype(F32)
    y_own[...] = y.astype(BF16)

    def g_copy(d):
        dev = lax.rem(s + d, n)
        return remote(y_own, out_all.at[s], g_s.at[dev], g_r.at[s], dev)

    for d in range(1, n):
        g_copy(d).start()
    out_ref[:, pl.ds(pl.multiple_of(s * yw, yw), yw)] = y_own[...]
    for d in range(1, n):
        src = lax.rem(s + d, n)
        remote(y_own, out_all.at[src], g_s.at[src], g_r.at[src], src).wait_recv()
        out_ref[:, pl.ds(pl.multiple_of(src * yw, yw), yw)] = out_all[src]

    for t in range(3):
        ag_done(t)

    @pl.loop(0, nch)
    def _(k):
        d2d_copy(k).wait_send()
        for cp in hop_copies(k) + mid_copies(k):
            cp.wait_send()

    for d in range(1, n):
        y_copy(d).wait_send()
        g_copy(d).wait_send()


def solution(mesh):
    n = mesh.shape['seq']
    row_spec = P('batch', None)
    cache_spec = P('batch', 'seq', None)
    in_specs = (row_spec, P('batch'), cache_spec, cache_spec, P(None, 'seq', None), P(None, 'seq', None),
                P('seq', None, None), P('seq', None, None), P('seq', None, None))

    def mla_step(hidden, lengths, c_kv, k_rope, w_uq, w_qr, w_uk, w_uv, w_o):
        rows, dm = hidden.shape
        t_len, lat = c_kv.shape[1:]
        rope = k_rope.shape[2]
        nh, nope = w_uq.shape[1:]
        vdim = w_uv.shape[2]
        scale = 1.0 / math.sqrt(nope + rope)
        nch, yw, width = rows // RPC, dm // n, RPC * lat + 128
        any_spec = pl.BlockSpec(memory_space=pl.ANY)
        vmem = pl.BlockSpec(memory_space=pltpu.VMEM)
        dma, V = pltpu.SemaphoreType.DMA, pltpu.VMEM
        return pl.pallas_call(
            functools.partial(kernel, n, scale),
            out_shape=jax.ShapeDtypeStruct((rows, dm), BF16),
            in_specs=[pl.BlockSpec(memory_space=pltpu.SMEM), vmem] + [any_spec] * 7,
            out_specs=vmem,
            scratch_shapes=[
                V((rows, dm * 8), BF16), V((SLOTS, DCH, 8, nope), BF16), V((2, 8 * nope, lat), BF16),
                V((2, 8 * lat, vdim), BF16), V((nh * vdim, dm), BF16), V((rows, t_len, lat), BF16),
                V((rows, rope, t_len), BF16), V((128, nope), F32), V((n, 2, 128, lat), BF16),
                V((128, 128), BF16), V((n, 128, 128), BF16), V((RPC, nh * n, lat), BF16),
                V((nch, 2, n // 2, 2, 8, width), F32), V((nch, n // 2, 2, 8, width), F32),
                V((nch, 2, 8, width), F32), V((nch, 4, 8, width), F32), V((2, 128, lat), BF16),
                V((rows, nh * vdim), BF16), V((n, rows, yw), F32), V((n, rows, yw), F32),
                V((rows, yw), BF16), V((n, rows, yw), BF16),
                dma((SLOTS,)), dma((2,)), dma((8,)), dma((rows,)), dma((rows,)), dma(()), dma((8,)),
                dma((3, 7)), dma((3, n)), dma((nch, 7)), dma((nch,)), dma((nch, 2)), dma((nch, 4)),
                dma((n,)), dma((n,)), dma((n,)), dma((n,)),
            ],
            compiler_params=pltpu.CompilerParams(collective_id=0, has_side_effects=True,
                                                 vmem_limit_bytes=67043328),
        )(lengths, hidden, c_kv, jnp.swapaxes(k_rope, 1, 2), w_uq.reshape(dm, 2, nh // 2, nope),
          jnp.transpose(w_qr, (1, 2, 0)).reshape(nh * rope, dm), w_uk.reshape(2, nh // 2 * nope, lat),
          w_uv.reshape(2, nh // 2 * lat, vdim), w_o.reshape(nh * vdim, dm))

    return jax.shard_map(mla_step, mesh=mesh, in_specs=in_specs, out_specs=row_spec, check_vma=False)
```

time: 225 us -> 85.8 us (0.38)
  waiting for transfers between devices: 117 us -> 0 us
  Pallas kernels: 0 us -> 84.1 us
  matrix products: 60.9 us -> 0 us
  other arithmetic: 16.6 us -> 0 us
  between operations: 13.3 us -> 0.01 us
  blocking collectives: 12.5 us -> 0 us
    pallas_call x0 -> x1, Pallas kernels: none -> 84.1 us  [mla_step(): pl.pallas_call(functools.partial(kernel, n, scale), out_shape=jax.ShapeDt...]
    dot_general x6 -> x0, matrix products: 60.9 us -> none  [the longest x1 13.9 us: mla_step(): jnp.einsum('bht,btc->bhc', p_weights.astype(jnp.bfloat16), c_kv, preferre...]
    psum x1 -> x0, waiting for transfers between devices: 54.2 us -> none  [mla_step(): y_sum = lax.psum(y_part, 'seq')]
    reduce_scatter x1 -> x0, waiting for transfers between devices: 34.8 us -> none  [mla_step(): merged = lax.psum_scatter(packed, 'seq', scatter_dimension=1, tiled=True)]
    all_gather x1 -> x0, waiting for transfers between devices: 27.5 us -> none  [mla_step(): q_all = lax.all_gather(q_local, 'seq', axis=1, tiled=True)]
    pmax x1 -> x0, blocking collectives: 12.5 us -> none  [mla_step(): global_max = lax.pmax(local_max, 'seq')]
    reduce_sum x1 -> x0, other arithmetic: 7.7 us -> none  [mla_step(): weight_sum = jnp.sum(p_weights, axis=2)]
    concatenate x2 -> x0, other arithmetic: 5.81 us -> none  [the longest x1 5.05 us: mla_step(): jnp.concatenate([latent_sum * rescale[:, :, None], (weight_sum * rescale)...]
  transfers between devices with their start and end apart: 3 -> 0, of which waited for: 3 -> 0; matrix products, arithmetic and copies ran while one was open for 0% -> 0% of each run, Pallas kernels for 0% -> 0%
where the time goes in v1:
time: 85.8 us; the launch traced here: 85.7 us
  Pallas kernels  84.1 us (98%)
  local copies, waits for them, and re-layouts  1.59 us (2%)
    pallas_call x1, Pallas kernels, mla_step(): pl.pallas_call(functools.partial(kernel, n, scale), out_shape=jax.ShapeDt...  84.1 us

profile of v1, /device:TPU:81, one launch (start us, length us, event | category | flops | bytes accessed | tf_op | source)
XLA Modules:
  0.0 85.7 jit_solution(9182473693476870117)
XLA Ops:
  0.0 84.1 %shard_map.91 = bf16[16,5120]{1,0:T(8,128)(2,1)} custom-call(s32[16]{0:T(128)} %lens.1, bf16[16,5120]{1,0:T(8,128)(2,1)} %hid.1, bf16[16,1024,512]{2,1,0:T(8,128)(2,1)} %c_hbm.1, bf16[16,64,1024]{2,1,0:T(8,128)(2,1)} %bitcast.11, bf16[5120,2,8,128]{3,2,1,0:T(8,128)(2,1)} %bitcast.8, bf16[1024,5120]{1,0:T(8,128)(2,1)} %bitcast.10, ...), custom_call_target="tpu_custom_call" | custom-call | tf_op jit(solution)/shard_map/pallas_call | solution.py:422
  84.1 1.6 %copy.11 = bf16[16,5120]{1,0:T(8,128)(2,1)} copy(bf16[16,5120]{1,0:T(8,128)(2,1)} %shard_map.91) | data formatting | bytes 327680

commit v2 on v1

--- a/solution.py
+++ b/solution.py
@@ -12,8 +12,8 @@
 F32 = jnp.float32
 BF16 = jnp.bfloat16
 LOWEST = float(jnp.finfo(jnp.float32).min)
-DCH = 256
-SLOTS = 8
+DCH = 512
+SLOTS = 4
 RPC = 2
 
 
@@ -53,11 +53,11 @@
     return out
 
 
-def kernel(n, scale, lens, hid, c_hbm, k_hbm, wuq_hbm, wqr_hbm, wuk_hbm, wuv_hbm, wo_hbm, out_ref,
-           hexp, wbuf, wuk, wuv, wo, cb, kb, acc, q_all, qr_st, qr_all, qrow, o_buf, d2d, mid, fin, ol, ovb,
-           y_send, y_recv, y_own, out_all,
-           w_sem, wuk_sem, wqr_sem, c_sem, k_sem, wuv_sem, wo_sem,
-           ag_s, ag_r, rs_s, d2d_r, mid_r, fin_r, y_s, y_r, g_s, g_r):
+def kernel(n, scale, lens, hid_hbm, c_hbm, k_hbm, wuq_hbm, wqr_hbm, wuk_hbm, wuv_hbm, wo_hbm, out_ref,
+           hid, hexp, wbuf, wuk, wuv, wo, cb, kb, acc, q_all, qr_st, qr_all, qrow, o_buf, d2d, mid, fin, ol, ovb,
+           y_send, y_pair, y_recv, y_own, out_all,
+           hid_sem, w_sem, wuk_sem, wqr_sem, c_sem, k_sem, wuv_sem, wo_sem,
+           ag_s, ag_r, rs_s, d2d_r, mid_r, fin_r, yp_s, yp_r, y_s, y_r, g_s, g_r):
     s = lax.axis_index("seq")
     x, c = lax.div(s, 2), lax.rem(s, 2)
     nx = n // 2
@@ -94,14 +94,17 @@
     def wo_copy(j):
         return pltpu.make_async_copy(wo_hbm.at[pl.ds(j * 256, 256)], wo.at[pl.ds(j * 256, 256)], wo_sem.at[j])
 
-    wuk_copy(0).start()
+    hid_copy = pltpu.make_async_copy(hid_hbm, hid, hid_sem)
+    hid_copy.start()
     for g in range(SLOTS):
         w_copy(jnp.int32(g)).start()
+    wuk_copy(0).start()
 
     barrier = pltpu.get_barrier_semaphore()
     for d in range(1, n):
         pl.semaphore_signal(barrier, inc=1, device_id={"seq": lax.rem(s + d, n)}, device_id_type=MESH)
 
+    hid_copy.wait()
     rep = jnp.where(iota((128, 1024), 0) == lax.div(iota((128, 1024), 1), 8), 1.0, 0.0).astype(BF16)
     ndt = dm // 128
     for g0 in range(0, ndt, 8):
@@ -117,34 +120,40 @@
     to_hb = jnp.where(ci == lax.rem(ri, 16) * 8 + lax.div(ri, 16), 1.0, 0.0).astype(BF16)
     row_h = lax.rem(iota((128, 1), 0), 8)
 
-    pl.semaphore_wait(barrier, n - 1)
+    opp = 2 * xo + c
 
     def ag_buf(t, owner):
-        return qr_all.at[owner] if t == 2 else q_all.at[owner, t]
+        return qr_all.at[owner] if t == 4 else q_all.at[owner, t // 2, pl.ds(t % 2 * 64, 64)]
 
     def ag(t, i, owner, dev):
         return remote(ag_buf(t, owner), ag_buf(t, owner), ag_s.at[t, i], ag_r.at[t, owner], dev)
 
-    def ag_own(t):
-        ag(t, 0, s, right).start()
-        ag(t, 1, s, left).start()
-        ag(t, 2, s, partner).start()
-
-    def ag_fwd1(t):
-        ag(t, 0, left, right).wait_recv()
-        ag(t, 3, left, partner).start()
-        if t != 1:
-            ag(t, 5, left, right).start()
-        ag(t, 1, right, left).wait_recv()
-        ag(t, 4, right, partner).start()
-        if t == 1:
-            ag(t, 5, right, left).start()
-
-    opp = 2 * xo + c
-
-    def ag_fwd2(t):
-        ag(t, 5, opp, right).wait_recv()
-        ag(t, 6, opp, partner).start()
+    def ag_own(half):
+        t0, t1 = 2 * half, 2 * half + 1
+        for t, i, dev in ((t0, 0, right), (t1, 1, left), (t1, 0, right), (t0, 1, left), (t0, 2, partner),
+                          (t1, 2, partner)):
+            ag(t, i, s, dev).start()
+
+    def ag_fwd1(half):
+        t0, t1 = 2 * half, 2 * half + 1
+        ag(t0, 0, left, right).wait_recv()
+        ag(t0, 5, left, right).start()
+        ag(t0, 3, left, partner).start()
+        ag(t1, 1, right, left).wait_recv()
+        ag(t1, 5, right, left).start()
+        ag(t1, 4, right, partner).start()
+
+    def ag_fwd2(half):
+        t0, t1 = 2 * half, 2 * half + 1
+        ag(t1, 0, left, right).wait_recv()
+        ag(t1, 3, left, partner).start()
+        ag(t0, 1, right, left).wait_recv()
+        ag(t0, 4, right, partner).start()
+
+    def ag_fwd3(half):
+        for t in (2 * half, 2 * half + 1):
+            ag(t, 5, opp, right).wait_recv()
+            ag(t, 6, opp, partner).start()
 
     def ag_partner(t):
         for xx in (x, xl, xr, xo):
@@ -175,22 +184,19 @@
             def _():
                 w_copy(g + SLOTS).start()
 
-            @pl.when(g >= 2 * nc - 8)
+            @pl.when(g >= 2 * nc - SLOTS)
             def _():
-                wqr_copy(g - (2 * nc - 8)).start()
+                for e in range(8 // SLOTS):
+                    wqr_copy((g - (2 * nc - SLOTS)) * (8 // SLOTS) + e).start()
 
             if half == 0:
-                @pl.when(i == 4)
+                @pl.when(i == 1)
                 def _():
                     wuk_copy(1).start()
             else:
-                @pl.when(i == nc // 2 + 2)
+                @pl.when(i == nc - 1)
                 def _():
                     ag_fwd1(0)
-
-                @pl.when(i == nc - 1)
-                def _():
-                    ag_fwd2(0)
 
         qn = dot(to_bh, acc[...].astype(BF16)).astype(BF16)
         wuk_copy(half).wait()
@@ -198,6 +204,8 @@
         for h in range(8):
             ql += dot(jnp.where(row_h == h, qn, jnp.zeros_like(qn)), wuk[half, h * 128:(h + 1) * 128, :])
         q_all[s, half] = ql.astype(BF16)
+        if half == 0:
+            pl.semaphore_wait(barrier, n - 1)
         ag_own(half)
 
     half_step(0)
@@ -213,17 +221,25 @@
             c_copy(b).start()
             k_copy(b).start()
 
-        @pl.when(j == 5)
-        def _():
-            ag_fwd1(1)
+        @pl.when(j == 2)
+        def _():
+            ag_fwd2(0)
+
+        @pl.when(j == 6)
+        def _():
+            ag_fwd3(0)
 
     qr_all[s] = dot(to_bh, qr_st[...]).astype(BF16)
-    ag_own(2)
+    for i, dev in ((0, right), (1, left), (5, opp), (2, partner)):
+        ag(4, i, s, dev).start()
     pltpu.make_async_copy(wuv_hbm, wuv, wuv_sem).start()
+    ag_fwd1(1)
     ag_fwd2(1)
-    ag_fwd1(2)
-    ag_fwd2(2)
-    for t in range(3):
+    for i, owner in ((3, left), (4, right), (6, opp)):
+        ag(4, 0, owner, right).wait_recv()
+        ag(4, i, owner, partner).start()
+    ag_fwd3(1)
+    for t in range(5):
         ag_partner(t)
 
     dup = jnp.where(lax.div(iota((128, 64), 0), 2) == iota((128, 64), 1), 1.0, 0.0).astype(BF16)
@@ -317,7 +333,7 @@
             ol[ab, pl.ds(pl.multiple_of(k * 16, 16), 16), :] = jnp.concatenate(
                 [o / l for o, _, l in res], axis=0).astype(BF16)
 
-    @pl.loop(0, nch + 3)
+    @pl.loop(0, nch + 5)
     def _(k):
         @pl.when(k < nch)
         def _():
@@ -329,13 +345,13 @@
         def _():
             pair_stage(k - 1)
 
-        @pl.when((k >= 2) & (k < nch + 2))
-        def _():
-            mid_stage(k - 2)
-
-        @pl.when(k >= 3)
-        def _():
-            final_stage(k - 3)
+        @pl.when((k >= 3) & (k < nch + 3))
+        def _():
+            mid_stage(k - 3)
+
+        @pl.when(k >= 5)
+        def _():
+            final_stage(k - 5)
 
     pltpu.make_async_copy(wuv_hbm, wuv, wuv_sem).wait()
     for ab in range(2):
@@ -351,27 +367,36 @@
 
     yw = dm // n
 
-    def y_copy(d):
-        dev = lax.rem(s + d, n)
-        return remote(y_send.at[dev], y_recv.at[s], y_s.at[dev], y_r.at[s], dev)
-
-    def y_wait(src):
-        return remote(y_send.at[src], y_recv.at[src], y_s.at[src], y_r.at[src], src)
-
-    @pl.loop(1, n + 1)
-    def _(d):
-        dev = lax.rem(s + d, n)
-        y_send[dev] = dot(ovb[...], wo[:, pl.ds(pl.multiple_of(dev * yw, yw), yw)])
-
-        @pl.when(d < n)
-        def _():
-            y_copy(d).start()
+    def y_block(p):
+        return dot(ovb[...], wo[:, pl.ds(pl.multiple_of(p * yw, yw), yw)])
+
+    def yp_copy(xx):
+        return remote(y_send.at[2 * xx + oc], y_pair.at[xx], yp_s.at[xx], yp_r.at[xx], partner)
+
+    def y_copy(xx):
+        return remote(y_send.at[2 * xx + c], y_recv.at[x], y_s.at[xx], y_r.at[x], 2 * xx + c)
+
+    @pl.loop(0, nx)
+    def _(i):
+        xx = lax.rem(x + nx - 1 - i, nx)
+        y_send[2 * xx + oc] = y_block(2 * xx + oc)
+        yp_copy(xx).start()
+
+    @pl.loop(0, nx)
+    def _(i):
+        xx = lax.rem(x + nx - 1 - i, nx)
+        blk = y_block(2 * xx + c)
+        yp_copy(xx).wait_recv()
+        y_send[2 * xx + c] = blk + y_pair[xx]
+
+        @pl.when(i < nx - 1)
+        def _():
+            y_copy(xx).start()
 
     y = y_send[s]
-    for d in range(1, n):
-        src = lax.rem(s + d, n)
-        y_wait(src).wait_recv()
-        y += y_recv[src]
+    for xx in (xr, xl, xo):
+        remote(y_send.at[s], y_recv.at[xx], y_s.at[xx], y_r.at[xx], right).wait_recv()
+        y += y_recv[xx]
     y += hid[:, pl.ds(pl.multiple_of(s * yw, yw), yw)].astype(F32)
     y_own[...] = y.astype(BF16)
 
@@ -387,7 +412,7 @@
         remote(y_own, out_all.at[src], g_s.at[src], g_r.at[src], src).wait_recv()
         out_ref[:, pl.ds(pl.multiple_of(src * yw, yw), yw)] = out_all[src]
 
-    for t in range(3):
+    for t in range(5):
         ag_done(t)
 
     @pl.loop(0, nch)
@@ -396,8 +421,11 @@
         for cp in hop_copies(k) + mid_copies(k):
             cp.wait_send()
 
+    for xx in range(nx):
+        yp_copy(xx).wait_send()
+    for xx in (xr, xl, xo):
+        y_copy(xx).wait_send()
     for d in range(1, n):
-        y_copy(d).wait_send()
         g_copy(d).wait_send()
 
 
@@ -422,20 +450,20 @@
         return pl.pallas_call(
             functools.partial(kernel, n, scale),
             out_shape=jax.ShapeDtypeStruct((rows, dm), BF16),
-            in_specs=[pl.BlockSpec(memory_space=pltpu.SMEM), vmem] + [any_spec] * 7,
+            in_specs=[pl.BlockSpec(memory_space=pltpu.SMEM)] + [any_spec] * 8,
             out_specs=vmem,
             scratch_shapes=[
-                V((rows, dm * 8), BF16), V((SLOTS, DCH, 8, nope), BF16), V((2, 8 * nope, lat), BF16),
+                V((rows, dm), BF16), V((rows, dm * 8), BF16), V((SLOTS, DCH, 8, nope), BF16), V((2, 8 * nope, lat), BF16),
                 V((2, 8 * lat, vdim), BF16), V((nh * vdim, dm), BF16), V((rows, t_len, lat), BF16),
                 V((rows, rope, t_len), BF16), V((128, nope), F32), V((n, 2, 128, lat), BF16),
                 V((128, 128), BF16), V((n, 128, 128), BF16), V((RPC, nh * n, lat), BF16),
                 V((nch, 2, n // 2, 2, 8, width), F32), V((nch, n // 2, 2, 8, width), F32),
                 V((nch, 2, 8, width), F32), V((nch, 4, 8, width), F32), V((2, 128, lat), BF16),
-                V((rows, nh * vdim), BF16), V((n, rows, yw), F32), V((n, rows, yw), F32),
+                V((rows, nh * vdim), BF16), V((n, rows, yw), F32), V((n // 2, rows, yw), F32), V((n // 2, rows, yw), F32),
                 V((rows, yw), BF16), V((n, rows, yw), BF16),
-                dma((SLOTS,)), dma((2,)), dma((8,)), dma((rows,)), dma((rows,)), dma(()), dma((8,)),
-                dma((3, 7)), dma((3, n)), dma((nch, 7)), dma((nch,)), dma((nch, 2)), dma((nch, 4)),
-                dma((n,)), dma((n,)), dma((n,)), dma((n,)),
+                dma(()), dma((SLOTS,)), dma((2,)), dma((8,)), dma((rows,)), dma((rows,)), dma(()), dma((8,)),
+                dma((5, 7)), dma((5, n)), dma((nch, 7)), dma((nch,)), dma((nch, 2)), dma((nch, 4)),
+                dma((n // 2,)), dma((n // 2,)), dma((n // 2,)), dma((n // 2,)), dma((n,)), dma((n,)),
             ],
             compiler_params=pltpu.CompilerParams(collective_id=0, has_side_effects=True,
                                                  vmem_limit_bytes=67043328),

time: 85.8 us -> 72.8 us (0.85)
  Pallas kernels: 84.1 us -> 71.1 us
    pallas_call x1, Pallas kernels: 84.1 us -> 71.1 us  [mla_step(): pl.pallas_call(functools.partial(kernel, n, scale), out_shape=jax.ShapeDt...]
where the time goes in v2:
time: 72.8 us; the launch traced here: 72.7 us
  Pallas kernels  71.1 us (98%)
  local copies, waits for them, and re-layouts  1.59 us (2%)
    pallas_call x1, Pallas kernels, mla_step(): pl.pallas_call(functools.partial(kernel, n, scale), out_shape=jax.ShapeDt...  71.1 us
    unnamed x1, local copies, waits for them, and re-layouts  1.59 us

profile of v2, /device:TPU:81, one launch (start us, length us, event | category | flops | bytes accessed | tf_op | source)
XLA Modules:
  0.0 72.7 jit_solution(16223968703027961187)
XLA Ops:
  0.0 71.1 %shard_map.91 = bf16[16,5120]{1,0:T(8,128)(2,1)} custom-call(s32[16]{0:T(128)} %lens.1, bf16[16,5120]{1,0:T(8,128)(2,1)} %hid_hbm.1, bf16[16,1024,512]{2,1,0:T(8,128)(2,1)} %c_hbm.1, bf16[16,64,1024]{2,1,0:T(8,128)(2,1)} %bitcast.11, bf16[5120,2,8,128]{3,2,1,0:T(8,128)(2,1)} %bitcast.8, bf16[1024,5120]{1,0:T(8,128)(2,1)} %bitcast.10, ...), custom_call_target="tpu_custom_call" | custom-call | tf_op jit(solution)/shard_map/pallas_call | solution.py:450
  71.1 1.6 %copy.11 = bf16[16,5120]{1,0:T(8,128)(2,1)} copy(bf16[16,5120]{1,0:T(8,128)(2,1)} %shard_map.91) | data formatting | bytes 327680

commit v3 on v2

--- a/solution.py
+++ b/solution.py
@@ -14,6 +14,7 @@
 LOWEST = float(jnp.finfo(jnp.float32).min)
 DCH = 512
 SLOTS = 4
+KST = 1024
 RPC = 2
 
 
@@ -57,7 +58,7 @@
            hid, hexp, wbuf, wuk, wuv, wo, cb, kb, acc, q_all, qr_st, qr_all, qrow, o_buf, d2d, mid, fin, ol, ovb,
            y_send, y_pair, y_recv, y_own, out_all,
            hid_sem, w_sem, wuk_sem, wqr_sem, c_sem, k_sem, wuv_sem, wo_sem,
-           ag_s, ag_r, rs_s, d2d_r, mid_r, fin_r, yp_s, yp_r, y_s, y_r, g_s, g_r):
+           ag_s, ag_r, d2d_s, rs_s, d2d_r, mid_r, fin_r, yp_s, yp_r, y_s, y_r, g_s, g_r):
     s = lax.axis_index("seq")
     x, c = lax.div(s, 2), lax.rem(s, 2)
     nx = n // 2
@@ -167,34 +168,37 @@
     def half_step(half):
         acc[...] = jnp.zeros_like(acc)
 
-        @pl.loop(0, nc)
-        def _(i):
-            g = half * nc + i
-            slot = lax.rem(g, SLOTS)
-            w_copy(g).wait()
-            wv = wbuf[slot].reshape(kk, 128)
+        @pl.loop(0, nc // 2)
+        def _(i2):
             part = acc[...]
-            for q0 in range(0, kk, 512):
-                hx = hexp[:, pl.ds(pl.multiple_of(i * kk + q0, 512), 512)]
-                lhs = jnp.concatenate([hx] * 8, axis=0) * jnp.concatenate([head_mask] * 4, axis=1)
-                part += dot(lhs, wv[q0:q0 + 512])
+            for u in range(2):
+                i = 2 * i2 + u
+                g = half * nc + i
+                w_copy(g).wait()
+                wv = wbuf[lax.rem(g, SLOTS)].reshape(kk, 128)
+                for q0 in range(0, kk, KST):
+                    hx = hexp[:, pl.ds(pl.multiple_of(i * kk + q0, KST), KST)]
+                    lhs = jnp.concatenate([hx] * 8, axis=0) * jnp.concatenate([head_mask] * (KST // 128), axis=1)
+                    part += dot(lhs, wv[q0:q0 + KST])
             acc[...] = part
-
-            @pl.when(g + SLOTS < 2 * nc)
+            g0 = half * nc + 2 * i2
+
+            @pl.when(g0 + SLOTS < 2 * nc)
             def _():
-                w_copy(g + SLOTS).start()
-
-            @pl.when(g >= 2 * nc - SLOTS)
+                w_copy(g0 + SLOTS).start()
+                w_copy(g0 + SLOTS + 1).start()
+
+            @pl.when(g0 >= 2 * nc - SLOTS)
             def _():
-                for e in range(8 // SLOTS):
-                    wqr_copy((g - (2 * nc - SLOTS)) * (8 // SLOTS) + e).start()
+                for e in range(16 // SLOTS):
+                    wqr_copy((g0 - (2 * nc - SLOTS)) * (8 // SLOTS) + e).start()
 
             if half == 0:
-                @pl.when(i == 1)
+                @pl.when(i2 == 0)
                 def _():
                     wuk_copy(1).start()
             else:
-                @pl.when(i == nc - 1)
+                @pl.when(i2 == nc // 2 - 1)
                 def _():
                     ag_fwd1(0)
 
@@ -214,8 +218,8 @@
     @pl.loop(0, 8)
     def _(j):
         wqr_copy(j).wait()
-        qr = dot_nt(hid[...], wo[pl.ds(pl.multiple_of(j * 128, 128), 128), :])
-        qr_st[pl.ds(pl.multiple_of(j * 16, 16), 16), :] = qr.astype(BF16)
+        qr = dot_nt(wo[pl.ds(pl.multiple_of(j * 128, 128), 128), :], hid[...])
+        qr_st[pl.ds(pl.multiple_of(j * 16, 16), 16), :] = qr.T.astype(BF16)
         for r in range(2):
             b = 2 * j + r
             c_copy(b).start()
@@ -282,21 +286,23 @@
                 o_buf[k, p % 2, p // 2, ab, :, RPC * lat:] = ml[h0:h0 + 8]
 
     def d2d_copy(k):
-        return remote(o_buf.at[k, oc], d2d.at[k], rs_s.at[k, 0], d2d_r.at[k], partner)
-
-    def hop_copies(k):
-        return [
-            remote(o_buf.at[k, c, xo, 1], mid.at[k, 0], rs_s.at[k, 1], mid_r.at[k, 0], right),
-            remote(o_buf.at[k, c, xo, 0], mid.at[k, 1], rs_s.at[k, 2], mid_r.at[k, 1], left),
-            remote(o_buf.at[k, c, xr, 0], fin.at[k, 0], rs_s.at[k, 3], fin_r.at[k, 0], right),
-            remote(o_buf.at[k, c, xl, 1], fin.at[k, 1], rs_s.at[k, 4], fin_r.at[k, 1], left),
-        ]
-
-    def mid_copies(k):
-        return [
-            remote(o_buf.at[k, c, xr, 1], fin.at[k, 2], rs_s.at[k, 5], fin_r.at[k, 2], right),
-            remote(o_buf.at[k, c, xl, 0], fin.at[k, 3], rs_s.at[k, 6], fin_r.at[k, 3], left),
-        ]
+        return remote(o_buf.at[k, oc], d2d.at[k], d2d_s.at[k], d2d_r.at[k], partner)
+
+    def sides(k):
+        turn = 1 - 2 * lax.rem(k, 2)
+        return lax.rem(x + nx + turn, nx), lax.rem(x + nx - turn, nx)
+
+    def far_copy(ab, k):
+        xp, _ = sides(k)
+        return remote(o_buf.at[k, c, xo, ab], mid.at[k, ab], rs_s.at[k, ab, 0], mid_r.at[k, ab], 2 * xp + c)
+
+    def near_copy(ab, k):
+        _, xq = sides(k)
+        return remote(o_buf.at[k, c, xq, ab], fin.at[k, ab, 0], rs_s.at[k, ab, 1], fin_r.at[k, ab, 0], 2 * xq + c)
+
+    def mid_copy(ab, k):
+        xp, _ = sides(k)
+        return remote(o_buf.at[k, c, xp, ab], fin.at[k, ab, 1], rs_s.at[k, ab, 2], fin_r.at[k, ab, 1], 2 * xp + c)
 
     def store_merged(k, xx, ab, other):
         ref = o_buf.at[k, c, xx, ab]
@@ -307,33 +313,30 @@
 
     def pair_stage(k):
         d2d_copy(k).wait_recv()
-        for xx in range(nx):
-            for ab in range(2):
+        for ab in range(2):
+            for xx in range(nx):
                 store_merged(k, xx, ab, d2d[k, xx, ab])
-        for cp in hop_copies(k):
-            cp.start()
-
-    def mid_stage(k):
-        hops, mids = hop_copies(k), mid_copies(k)
-        hops[0].wait_recv()
-        store_merged(k, xr, 1, mid[k, 0])
-        mids[0].start()
-        hops[1].wait_recv()
-        store_merged(k, xl, 0, mid[k, 1])
-        mids[1].start()
-
-    def final_stage(k):
-        hops, mids = hop_copies(k), mid_copies(k)
-        hops[2].wait_recv()
-        hops[3].wait_recv()
-        mids[0].wait_recv()
-        mids[1].wait_recv()
-        for ab, (f0, f1) in enumerate(((0, 3), (1, 2))):
-            res = merge([o_buf[k, c, x, ab], fin[k, f0], fin[k, f1]], lat)
-            ol[ab, pl.ds(pl.multiple_of(k * 16, 16), 16), :] = jnp.concatenate(
-                [o / l for o, _, l in res], axis=0).astype(BF16)
-
-    @pl.loop(0, nch + 5)
+
+    def hop(ab, k):
+        far_copy(ab, k).start()
+        near_copy(ab, k).start()
+
+    def mid_stage(ab, k):
+        xp, _ = sides(k)
+        far_copy(ab, k).wait_recv()
+        store_merged(k, xp, ab, mid[k, ab])
+        mid_copy(ab, k).start()
+
+    def final_stage(ab, k):
+        near_copy(ab, k).wait_recv()
+        mid_copy(ab, k).wait_recv()
+        res = merge([o_buf[k, c, x, ab], fin[k, ab, 0], fin[k, ab, 1]], lat)
+        ol[ab, pl.ds(pl.multiple_of(k * 16, 16), 16), :] = jnp.concatenate(
+            [o / l for o, _, l in res], axis=0).astype(BF16)
+
+    early2 = nch // 2
+
+    @pl.loop(0, nch + 1)
     def _(k):
         @pl.when(k < nch)
         def _():
@@ -341,34 +344,76 @@
             d2d_copy(k).start()
             wo_copy(k).start()
 
-        @pl.when((k >= 1) & (k < nch + 1))
+        @pl.when(k >= 1)
         def _():
             pair_stage(k - 1)
-
-        @pl.when((k >= 3) & (k < nch + 3))
-        def _():
-            mid_stage(k - 3)
+            hop(0, k - 1)
+
+            @pl.when(lax.rem(k, 2) == 1)
+            def _():
+                @pl.when(k < nch)
+                def _():
+                    hop(1, lax.div(k - 1, 2))
+
+        @pl.when(k >= 3)
+        def _():
+            mid_stage(0, k - 3)
+
+            @pl.when(lax.rem(k, 2) == 1)
+            def _():
+                mid_stage(1, lax.div(k - 3, 2))
 
         @pl.when(k >= 5)
         def _():
-            final_stage(k - 5)
+            final_stage(0, k - 5)
+
+    @pl.loop(early2, nch)
+    def _(k):
+        hop(1, k)
+
+    @pl.loop(nch - 2, nch)
+    def _(k):
+        mid_stage(0, k)
+
+    mid_stage(1, early2 - 1)
+
+    @pl.loop(nch - 4, nch)
+    def _(k):
+        final_stage(0, k)
 
     pltpu.make_async_copy(wuv_hbm, wuv, wuv_sem).wait()
-    for ab in range(2):
+    hrows = wo.shape[0] // 2
+    yw = dm // n
+
+    def values(ab):
         ov = jnp.zeros((128, 128), F32)
         src = ol[ab]
         for h in range(8):
             ov += dot(jnp.where(row_h == h, src, jnp.zeros_like(src)), wuv[ab, h * lat:(h + 1) * lat, :])
         ov = dot(to_hb, ov.astype(BF16)).astype(BF16)
         for h in range(8):
-            ovb[:, (ab * 8 + h) * 128:(ab * 8 + h + 1) * 128] = ov[h * 16:(h + 1) * 16]
+            ovb[ab, :, h * 128:(h + 1) * 128] = ov[h * 16:(h + 1) * 16]
+
+    def y_block(ab, p):
+        return dot(ovb[ab], wo[ab * hrows:(ab + 1) * hrows, pl.ds(pl.multiple_of(p * yw, yw), yw)])
+
+    values(0)
     for j in range(8):
         wo_copy(j).wait()
 
-    yw = dm // n
-
-    def y_block(p):
-        return dot(ovb[...], wo[:, pl.ds(pl.multiple_of(p * yw, yw), yw)])
+    @pl.loop(0, n)
+    def _(p):
+        y_send[p] = y_block(0, p)
+
+        @pl.when(p >= n - (nch - early2))
+        def _():
+            mid_stage(1, p - (n - nch))
+
+    @pl.loop(0, nch)
+    def _(k):
+        final_stage(1, k)
+
+    values(1)
 
     def yp_copy(xx):
         return remote(y_send.at[2 * xx + oc], y_pair.at[xx], yp_s.at[xx], yp_r.at[xx], partner)
@@ -379,13 +424,13 @@
     @pl.loop(0, nx)
     def _(i):
         xx = lax.rem(x + nx - 1 - i, nx)
-        y_send[2 * xx + oc] = y_block(2 * xx + oc)
+        y_send[2 * xx + oc] += y_block(1, 2 * xx + oc)
         yp_copy(xx).start()
 
     @pl.loop(0, nx)
     def _(i):
         xx = lax.rem(x + nx - 1 - i, nx)
-        blk = y_block(2 * xx + c)
+        blk = y_send[2 * xx + c] + y_block(1, 2 * xx + c)
         yp_copy(xx).wait_recv()
         y_send[2 * xx + c] = blk + y_pair[xx]
 
@@ -418,8 +463,9 @@
     @pl.loop(0, nch)
     def _(k):
         d2d_copy(k).wait_send()
-        for cp in hop_copies(k) + mid_copies(k):
-            cp.wait_send()
+        for ab in range(2):
+            for cp in (far_copy(ab, k), near_copy(ab, k), mid_copy(ab, k)):
+                cp.wait_send()
 
     for xx in range(nx):
         yp_copy(xx).wait_send()
@@ -458,11 +504,11 @@
                 V((rows, rope, t_len), BF16), V((128, nope), F32), V((n, 2, 128, lat), BF16),
                 V((128, 128), BF16), V((n, 128, 128), BF16), V((RPC, nh * n, lat), BF16),
                 V((nch, 2, n // 2, 2, 8, width), F32), V((nch, n // 2, 2, 8, width), F32),
-                V((nch, 2, 8, width), F32), V((nch, 4, 8, width), F32), V((2, 128, lat), BF16),
-                V((rows, nh * vdim), BF16), V((n, rows, yw), F32), V((n // 2, rows, yw), F32), V((n // 2, rows, yw), F32),
+                V((nch, 2, 8, width), F32), V((nch, 2, 2, 8, width), F32), V((2, 128, lat), BF16),
+                V((2, rows, nh * vdim // 2), BF16), V((n, rows, yw), F32), V((n // 2, rows, yw), F32), V((n // 2, rows, yw), F32),
                 V((rows, yw), BF16), V((n, rows, yw), BF16),
                 dma(()), dma((SLOTS,)), dma((2,)), dma((8,)), dma((rows,)), dma((rows,)), dma(()), dma((8,)),
-                dma((5, 7)), dma((5, n)), dma((nch, 7)), dma((nch,)), dma((nch, 2)), dma((nch, 4)),
+                dma((5, 7)), dma((5, n)), dma((nch,)), dma((nch, 2, 3)), dma((nch,)), dma((nch, 2)), dma((nch, 2, 2)),
                 dma((n // 2,)), dma((n // 2,)), dma((n // 2,)), dma((n // 2,)), dma((n,)), dma((n,)),
             ],
             compiler_params=pltpu.CompilerParams(collective_id=0, has_side_effects=True,

time: 72.8 us -> 79.7 us (1.095)
  Pallas kernels: 71.1 us -> 78 us
    pallas_call x1, Pallas kernels: 71.1 us -> 78 us  [mla_step(): pl.pallas_call(functools.partial(kernel, n, scale), out_shape=jax.ShapeDt...]
where the time goes in v3:
time: 79.7 us; the launch traced here: 79.6 us
  Pallas kernels  78 us (98%)
  local copies, waits for them, and re-layouts  1.59 us (2%)
    pallas_call x1, Pallas kernels, mla_step(): pl.pallas_call(functools.partial(kernel, n, scale), out_shape=jax.ShapeDt...  78 us

profile of v3, /device:TPU:81, one launch (start us, length us, event | category | flops | bytes accessed | tf_op | source)
XLA Modules:
  0.0 79.6 jit_solution(11541013306448476244)
XLA Ops:
  0.0 78.0 %shard_map.91 = bf16[16,5120]{1,0:T(8,128)(2,1)} custom-call(s32[16]{0:T(128)} %lens.1, bf16[16,5120]{1,0:T(8,128)(2,1)} %hid_hbm.1, bf16[16,1024,512]{2,1,0:T(8,128)(2,1)} %c_hbm.1, bf16[16,64,1024]{2,1,0:T(8,128)(2,1)} %bitcast.11, bf16[5120,2,8,128]{3,2,1,0:T(8,128)(2,1)} %bitcast.8, bf16[1024,5120]{1,0:T(8,128)(2,1)} %bitcast.10, ...), custom_call_target="tpu_custom_call" | custom-call | tf_op jit(solution)/shard_map/pallas_call | solution.py:496
  78.0 1.6 %copy.11 = bf16[16,5120]{1,0:T(8,128)(2,1)} copy(bf16[16,5120]{1,0:T(8,128)(2,1)} %shard_map.91) | data formatting | bytes 327680

commit v4 on v2

--- a/solution.py
+++ b/solution.py
@@ -12,7 +12,7 @@
 F32 = jnp.float32
 BF16 = jnp.bfloat16
 LOWEST = float(jnp.finfo(jnp.float32).min)
-DCH = 512
+DCH = 256
 SLOTS = 4
 RPC = 2
 
@@ -75,8 +75,7 @@
                                             device_id={"seq": dev}, device_id_type=MESH)
 
     def w_copy(g):
-        half, i = lax.div(g, nc), lax.rem(g, nc)
-        return pltpu.make_async_copy(wuq_hbm.at[pl.ds(i * DCH, DCH), half], wbuf.at[lax.rem(g, SLOTS)],
+        return pltpu.make_async_copy(wuq_hbm.at[pl.ds(g * DCH, DCH)], wbuf.at[lax.rem(g, SLOTS)],
                                      w_sem.at[lax.rem(g, SLOTS)])
 
     def wuk_copy(half):
@@ -98,7 +97,6 @@
     hid_copy.start()
     for g in range(SLOTS):
         w_copy(jnp.int32(g)).start()
-    wuk_copy(0).start()
 
     barrier = pltpu.get_barrier_semaphore()
     for d in range(1, n):
@@ -164,41 +162,37 @@
             ag(t, i, s, partner).wait_send()
 
     kk = DCH * 8
-    def half_step(half):
-        acc[...] = jnp.zeros_like(acc)
-
-        @pl.loop(0, nc)
-        def _(i):
-            g = half * nc + i
-            slot = lax.rem(g, SLOTS)
-            w_copy(g).wait()
-            wv = wbuf[slot].reshape(kk, 128)
-            part = acc[...]
-            for q0 in range(0, kk, 512):
-                hx = hexp[:, pl.ds(pl.multiple_of(i * kk + q0, 512), 512)]
-                lhs = jnp.concatenate([hx] * 8, axis=0) * jnp.concatenate([head_mask] * 4, axis=1)
-                part += dot(lhs, wv[q0:q0 + 512])
-            acc[...] = part
-
-            @pl.when(g + SLOTS < 2 * nc)
-            def _():
-                w_copy(g + SLOTS).start()
-
-            @pl.when(g >= 2 * nc - SLOTS)
-            def _():
-                for e in range(8 // SLOTS):
-                    wqr_copy((g - (2 * nc - SLOTS)) * (8 // SLOTS) + e).start()
-
-            if half == 0:
-                @pl.when(i == 1)
-                def _():
-                    wuk_copy(1).start()
-            else:
-                @pl.when(i == nc - 1)
-                def _():
-                    ag_fwd1(0)
-
-        qn = dot(to_bh, acc[...].astype(BF16)).astype(BF16)
+    acc[...] = jnp.zeros_like(acc)
+
+    @pl.loop(0, nc)
+    def _(g):
+        slot = lax.rem(g, SLOTS)
+        w_copy(g).wait()
+        w0 = wbuf[slot, :, 0].reshape(kk, 128)
+        w1 = wbuf[slot, :, 1].reshape(kk, 128)
+        part = acc[...]
+        for q0 in range(0, kk, 1024):
+            hx = hexp[:, pl.ds(pl.multiple_of(g * kk + q0, 1024), 1024)]
+            lhs = jnp.concatenate([hx] * 8, axis=0) * jnp.concatenate([head_mask] * 8, axis=1)
+            part += dot(lhs, jnp.concatenate([w0[q0:q0 + 1024], w1[q0:q0 + 1024]], axis=1))
+        acc[...] = part
+
+        @pl.when(g + SLOTS < nc)
+        def _():
+            w_copy(g + SLOTS).start()
+
+        @pl.when(g >= nc - SLOTS)
+        def _():
+            for e in range(8 // SLOTS):
+                wqr_copy((g - (nc - SLOTS)) * (8 // SLOTS) + e).start()
+
+        @pl.when(g == nc - 2 * SLOTS)
+        def _():
+            wuk_copy(0).start()
+            wuk_copy(1).start()
+
+    for half in range(2):
+        qn = dot(to_bh, acc[:, half * 128:(half + 1) * 128].astype(BF16)).astype(BF16)
         wuk_copy(half).wait()
         ql = jnp.zeros((128, lat), F32)
         for h in range(8):
@@ -207,9 +201,6 @@
         if half == 0:
             pl.semaphore_wait(barrier, n - 1)
         ag_own(half)
-
-    half_step(0)
-    half_step(1)
 
     @pl.loop(0, 8)
     def _(j):
@@ -221,23 +212,21 @@
             c_copy(b).start()
             k_copy(b).start()
 
-        @pl.when(j == 2)
-        def _():
-            ag_fwd2(0)
-
         @pl.when(j == 6)
         def _():
-            ag_fwd3(0)
+            ag_fwd1(0)
 
     qr_all[s] = dot(to_bh, qr_st[...]).astype(BF16)
     for i, dev in ((0, right), (1, left), (5, opp), (2, partner)):
         ag(4, i, s, dev).start()
     pltpu.make_async_copy(wuv_hbm, wuv, wuv_sem).start()
     ag_fwd1(1)
+    ag_fwd2(0)
     ag_fwd2(1)
     for i, owner in ((3, left), (4, right), (6, opp)):
         ag(4, 0, owner, right).wait_recv()
         ag(4, i, owner, partner).start()
+    ag_fwd3(0)
     ag_fwd3(1)
     for t in range(5):
         ag_partner(t)
@@ -453,9 +442,9 @@
             in_specs=[pl.BlockSpec(memory_space=pltpu.SMEM)] + [any_spec] * 8,
             out_specs=vmem,
             scratch_shapes=[
-                V((rows, dm), BF16), V((rows, dm * 8), BF16), V((SLOTS, DCH, 8, nope), BF16), V((2, 8 * nope, lat), BF16),
+                V((rows, dm), BF16), V((rows, dm * 8), BF16), V((SLOTS, DCH, 2, 8, nope), BF16), V((2, 8 * nope, lat), BF16),
                 V((2, 8 * lat, vdim), BF16), V((nh * vdim, dm), BF16), V((rows, t_len, lat), BF16),
-                V((rows, rope, t_len), BF16), V((128, nope), F32), V((n, 2, 128, lat), BF16),
+                V((rows, rope, t_len), BF16), V((128, 2 * nope), F32), V((n, 2, 128, lat), BF16),
                 V((128, 128), BF16), V((n, 128, 128), BF16), V((RPC, nh * n, lat), BF16),
                 V((nch, 2, n // 2, 2, 8, width), F32), V((nch, n // 2, 2, 8, width), F32),
                 V((nch, 2, 8, width), F32), V((nch, 4, 8, width), F32), V((2, 128, lat), BF16),

time: 72.8 us -> 73.9 us (1.015)
  Pallas kernels: 71.1 us -> 72.2 us
    pallas_call x1, Pallas kernels: 71.1 us -> 72.2 us  [mla_step(): pl.pallas_call(functools.partial(kernel, n, scale), out_shape=jax.ShapeDt...]
where the time goes in v4:
time: 73.9 us; the launch traced here: 73.8 us
  Pallas kernels  72.2 us (98%)
  local copies, waits for them, and re-layouts  1.59 us (2%)
    pallas_call x1, Pallas kernels, mla_step(): pl.pallas_call(functools.partial(kernel, n, scale), out_shape=jax.ShapeDt...  72.2 us
    unnamed x1, local copies, waits for them, and re-layouts  1.59 us

profile of v4, /device:TPU:81, one launch (start us, length us, event | category | flops | bytes accessed | tf_op | source)
XLA Modules:
  0.0 73.8 jit_solution(135107320737469369)
XLA Ops:
  0.0 72.2 %shard_map.91 = bf16[16,5120]{1,0:T(8,128)(2,1)} custom-call(s32[16]{0:T(128)} %lens.1, bf16[16,5120]{1,0:T(8,128)(2,1)} %hid_hbm.1, bf16[16,1024,512]{2,1,0:T(8,128)(2,1)} %c_hbm.1, bf16[16,64,1024]{2,1,0:T(8,128)(2,1)} %bitcast.11, bf16[5120,2,8,128]{3,2,1,0:T(8,128)(2,1)} %bitcast.8, bf16[1024,5120]{1,0:T(8,128)(2,1)} %bitcast.10, ...), custom_call_target="tpu_custom_call" | custom-call | tf_op jit(solution)/shard_map/pallas_call | solution.py:439
  72.2 1.6 %copy.11 = bf16[16,5120]{1,0:T(8,128)(2,1)} copy(bf16[16,5120]{1,0:T(8,128)(2,1)} %shard_map.91) | data formatting | bytes 327680

commit v5 on v2

--- a/solution.py
+++ b/solution.py
@@ -211,21 +211,22 @@
     half_step(0)
     half_step(1)
 
-    @pl.loop(0, 8)
+    @pl.loop(0, 4)
     def _(j):
-        wqr_copy(j).wait()
-        qr = dot_nt(hid[...], wo[pl.ds(pl.multiple_of(j * 128, 128), 128), :])
-        qr_st[pl.ds(pl.multiple_of(j * 16, 16), 16), :] = qr.astype(BF16)
-        for r in range(2):
-            b = 2 * j + r
+        wqr_copy(2 * j).wait()
+        wqr_copy(2 * j + 1).wait()
+        qr = dot_nt(hid[...], wo[pl.ds(pl.multiple_of(j * 256, 256), 256), :]).astype(BF16)
+        qr_st[pl.ds(pl.multiple_of(j * 32, 32), 32), :] = jnp.concatenate([qr[:, :128], qr[:, 128:]], axis=0)
+        for r in range(4):
+            b = 4 * j + r
             c_copy(b).start()
             k_copy(b).start()
 
-        @pl.when(j == 2)
+        @pl.when(j == 1)
         def _():
             ag_fwd2(0)
 
-        @pl.when(j == 6)
+        @pl.when(j == 3)
         def _():
             ag_fwd3(0)
 
@@ -370,6 +371,10 @@
     def y_block(p):
         return dot(ovb[...], wo[:, pl.ds(pl.multiple_of(p * yw, yw), yw)])
 
+    def chip_at(i):
+        q = lax.div(i, 2)
+        return lax.rem(x + (1 - q) * (2 + i) + q * (3 - i), nx)
+
     def yp_copy(xx):
         return remote(y_send.at[2 * xx + oc], y_pair.at[xx], yp_s.at[xx], yp_r.at[xx], partner)
 
@@ -378,13 +383,13 @@
 
     @pl.loop(0, nx)
     def _(i):
-        xx = lax.rem(x + nx - 1 - i, nx)
+        xx = chip_at(i)
         y_send[2 * xx + oc] = y_block(2 * xx + oc)
         yp_copy(xx).start()
 
     @pl.loop(0, nx)
     def _(i):
-        xx = lax.rem(x + nx - 1 - i, nx)
+        xx = chip_at(i)
         blk = y_block(2 * xx + c)
         yp_copy(xx).wait_recv()
         y_send[2 * xx + c] = blk + y_pair[xx]
@@ -400,15 +405,15 @@
     y += hid[:, pl.ds(pl.multiple_of(s * yw, yw), yw)].astype(F32)
     y_own[...] = y.astype(BF16)
 
-    def g_copy(d):
-        dev = lax.rem(s + d, n)
+    others = (2 * xo + c, 2 * xo + oc, right, left, 2 * xr + oc, 2 * xl + oc, partner)
+
+    def g_copy(dev):
         return remote(y_own, out_all.at[s], g_s.at[dev], g_r.at[s], dev)
 
-    for d in range(1, n):
-        g_copy(d).start()
+    for dev in others:
+        g_copy(dev).start()
     out_ref[:, pl.ds(pl.multiple_of(s * yw, yw), yw)] = y_own[...]
-    for d in range(1, n):
-        src = lax.rem(s + d, n)
+    for src in others:
         remote(y_own, out_all.at[src], g_s.at[src], g_r.at[src], src).wait_recv()
         out_ref[:, pl.ds(pl.multiple_of(src * yw, yw), yw)] = out_all[src]
 
@@ -425,8 +430,8 @@
         yp_copy(xx).wait_send()
     for xx in (xr, xl, xo):
         y_copy(xx).wait_send()
-    for d in range(1, n):
-        g_copy(d).wait_send()
+    for dev in others:
+        g_copy(dev).wait_send()
 
 
 def solution(mesh):

time: 72.8 us -> 72.1 us (level)
  no operation moved by 1% of the time
where the time goes in v5:
time: 72.1 us; the launch traced here: 72 us
  Pallas kernels  70.4 us (98%)
  local copies, waits for them, and re-layouts  1.59 us (2%)
    pallas_call x1, Pallas kernels, mla_step(): pl.pallas_call(functools.partial(kernel, n, scale), out_shape=jax.ShapeDt...  70.4 us
    unnamed x1, local copies, waits for them, and re-layouts  1.59 us

profile of v5, /device:TPU:81, one launch (start us, length us, event | category | flops | bytes accessed | tf_op | source)
XLA Modules:
  0.0 72.0 jit_solution(1703744516665674195)
XLA Ops:
  0.0 70.4 %shard_map.91 = bf16[16,5120]{1,0:T(8,128)(2,1)} custom-call(s32[16]{0:T(128)} %lens.1, bf16[16,5120]{1,0:T(8,128)(2,1)} %hid_hbm.1, bf16[16,1024,512]{2,1,0:T(8,128)(2,1)} %c_hbm.1, bf16[16,64,1024]{2,1,0:T(8,128)(2,1)} %bitcast.11, bf16[5120,2,8,128]{3,2,1,0:T(8,128)(2,1)} %bitcast.8, bf16[1024,5120]{1,0:T(8,128)(2,1)} %bitcast.10, ...), custom_call_target="tpu_custom_call" | custom-call | tf_op jit(solution)/shard_map/pallas_call | solution.py:455
  70.4 1.6 %copy.11 = bf16[16,5120]{1,0:T(8,128)(2,1)} copy(bf16[16,5120]{1,0:T(8,128)(2,1)} %shard_map.91) | data formatting | bytes 327680
